TPU v7x, 256 devices: a 4x2x16 block of a 4x16x16 slice. The times are simulated.
256 devices in a mesh: groups: 2 (over y), heads: 32 (over z, core), batch: 4 (over x).
Axes of the slice: x: 4, y: 2, z: 16, core: 2. Of those that a mesh axis runs over, the one named last changes fastest.
The devices are a block of a 4x16x16 slice.
Arguments:
- queries: bfloat16 [128, 8192], P(('groups', 'batch'), 'heads'), parts along dimension 0, may hold values from -110 to 110
- new_kv: bfloat16 [64, 64, 256], P(('groups', 'heads'), 'batch'), parts along dimension 0, may hold values from -15 to 15
- kv_pool: bfloat16 [64, 192, 128, 256], P(('groups', 'heads'), 'batch'), parts along dimension 0, may hold values from -6 to 6
- page_counts: int32 [8, 16], P(('groups', 'batch')), parts along dimension 0, may hold values from 1 to 6, 48 in all within a row
- last_fill: int32 [8, 16], P(('groups', 'batch')), parts along dimension 0, may hold values from 1 to 128
- page_order: int32 [8, 48], P(('groups', 'batch')), parts along dimension 0, may hold values from 0 to 47, each once within a row
- hidden: bfloat16 [128, 8192], P(('groups', 'batch')), parts along dimension 0, may hold values from -0.59765625 to 0.59765625
- out_weight: bfloat16 [8192, 8192], P('heads'), may hold values from -0.5 to 0.5
- norm_gain: bfloat16 [8192], replicated, may hold values from 0.099609375 to 1.8984375
- sectioned: bfloat16 [64, 4, 8, 128, 256], P(('groups', 'heads'), 'batch'), parts along dimension 0, may hold values from -6 to 6
- routes: int32 [64, 4, 8, 1], P(('groups', 'heads'), 'batch'), parts along dimension 0, may hold values from 0 to 7; in each aligned block of 8 rows (0 to 7, 8 to 15, ..., all dimensions but the last counted through in order) at most 2 rows name the same one
Outputs:
- residual_out: bfloat16 [128, 8192], P(('groups', 'batch')), parts along dimension 0
- normed: bfloat16 [128, 8192], P(('groups', 'batch')), parts along dimension 0
- arrival: bfloat16 [64, 4, 32, 2, 128, 256], P(('groups', 'heads'), 'batch'), parts along dimension 0
There are 2 independent parts, one for each index of `groups`. A program takes and returns all parts, laid end to end along the dimension named above; an argument that names none is the same for every part. Nothing has to cross between parts.
Inputs may be any that keep to these rules, and one draw needn't show every extreme that they name: `routes`: every key-value head is named by at most 2 sectioned pages of one device. `page_counts`: the page counts of one batch owner sum to 48.
All inputs are finite; a program needn't handle non-finite values.
Results may differ from a plain program's by a relative error of at most 0.0066.
Values may be sent and summed in bfloat16 or wider, within the bound.
A program may use at most 64 MiB of HBM per device.

v0:
```python
import functools

import jax
import jax.numpy as jnp
from jax import lax
from jax.experimental import pallas as pl
from jax.experimental.pallas import tpu as pltpu
from jax.sharding import PartitionSpec as P

KV_HEADS = 8
PER_HEAD_CAP = 2
CORES = 2
CHUNK_PAGES = 8
LANES = 128
PLAN = (
    "cw1",
    "ccw1",
    "tell2",
    "scores",
    "know2",
    "cw2",
    "ccw2",
    "tell4",
    "attention",
    "know4",
    "terms",
    "relay0",
    "relay1",
    "partner",
    "pair",
    "cw3",
    "ccw3",
    "relay2",
    "relay3",
    "sum",
    "block",
    "opposite",
    "far0",
    "far1",
    "far2",
    "far3",
    "relay4",
    "relay5",
    "brelay",
    "relay6",
    "share",
    "norm",
    "far4",
    "far5",
    "far6",
)
norm_epsilon = 1e-06

MESH = pl.DeviceIdType.MESH
F32 = jnp.float32
BF16 = jnp.bfloat16


def page_limits(counts_ref, fill_ref, order_ref, page_size):
    requests, pool = counts_ref.shape[1], order_ref.shape[1]
    lane = lax.broadcasted_iota(jnp.int32, (requests, requests), 1)
    row = lax.broadcasted_iota(jnp.int32, (requests, requests), 0)
    counts = jnp.broadcast_to(counts_ref[...].astype(F32), (requests, requests))
    fill = jnp.broadcast_to(fill_ref[...].astype(F32), (requests, requests))
    count_col = jnp.sum(jnp.where(lane == row, counts, 0.0), axis=1, keepdims=True)
    fill_col = jnp.sum(jnp.where(lane == row, fill, 0.0), axis=1, keepdims=True)
    ends = jnp.sum(jnp.where(lane <= row, counts, 0.0), axis=1, keepdims=True)
    starts = ends - count_col
    context = (count_col - 1.0) * page_size + fill_col
    place = lax.broadcasted_iota(jnp.int32, (requests, 128), 1).astype(F32)
    live = jnp.clip(context - page_size * (place - starts), 0.0, float(page_size))
    live = jnp.where((place >= starts) & (place < ends), live, 0.0)
    order = jnp.broadcast_to(order_ref[...], (pool, pool))
    lane = lax.broadcasted_iota(jnp.int32, (pool, pool), 1)
    row = lax.broadcasted_iota(jnp.int32, (pool, pool), 0)
    order_col = jnp.sum(jnp.where(lane == row, order.astype(F32), 0.0), axis=1, keepdims=True)
    page = lax.broadcasted_iota(jnp.int32, (pool, 128), 1).astype(F32)
    one_hot = jnp.where(order_col == page, 1.0, 0.0).astype(BF16)
    return jnp.dot(live[:, :pool].astype(BF16), one_hot, preferred_element_type=F32)


def attend_scores(q_ref, new_ref, kv, scores, limits):
    pool, page_size, width = kv.shape
    head_dim = width // 2
    requests = q_ref.shape[0]
    groups = q_ref.shape[1] // head_dim
    scale = 1.0 / head_dim**0.5
    q = jnp.concatenate([q_ref[:, g * head_dim : (g + 1) * head_dim] for g in range(groups)], axis=0)
    limits = jnp.concatenate([limits] * groups, axis=0)
    rows = groups * requests
    new_key = jnp.concatenate([new_ref[:, :head_dim].astype(F32)] * groups, axis=0)
    fresh = jnp.sum(q.astype(F32) * new_key, axis=1, keepdims=True) * scale
    token = lax.broadcasted_iota(jnp.int32, (rows, page_size), 1).astype(F32)
    top = jnp.full((rows, page_size), -1e30, F32)
    for first in range(0, pool, CHUNK_PAGES):
        keys = kv[first : first + CHUNK_PAGES, :, :head_dim].reshape(CHUNK_PAGES * page_size, head_dim)
        s = lax.dot_general(q, keys, (((1,), (1,)), ((), ())), preferred_element_type=F32) * scale
        for i in range(CHUNK_PAGES):
            part = s[:, i * page_size : (i + 1) * page_size]
            part = jnp.where(token < limits[:, first + i : first + i + 1], part, -1e30)
            top = jnp.maximum(top, part)
            scores[:, (first + i) * page_size : (first + i + 1) * page_size] = part
    return jnp.maximum(jnp.max(top, axis=1, keepdims=True), fresh), fresh


def attend_values(q_ref, new_ref, kv, scores, top, fresh):
    pool, page_size, width = kv.shape
    head_dim = width // 2
    requests = q_ref.shape[0]
    groups = q_ref.shape[1] // head_dim
    rows = groups * requests
    new_value = jnp.concatenate([new_ref[:, head_dim:].astype(F32)] * groups, axis=0)
    den = jnp.zeros((rows, page_size), F32)
    num = jnp.zeros((rows, head_dim), F32)
    for first in range(0, pool, CHUNK_PAGES):
        cols = slice(first * page_size, (first + CHUNK_PAGES) * page_size)
        w = jnp.exp(scores[:, cols] - top)
        for i in range(CHUNK_PAGES):
            den = den + w[:, i * page_size : (i + 1) * page_size]
        values = kv[first : first + CHUNK_PAGES, :, head_dim:].reshape(CHUNK_PAGES * page_size, head_dim)
        num = num + jnp.dot(w.astype(BF16), values, preferred_element_type=F32)
    fresh_w = jnp.exp(fresh - top)
    den = jnp.sum(den, axis=1, keepdims=True) + fresh_w
    num = num + fresh_w.astype(BF16).astype(F32) * new_value
    out = (num / den).astype(BF16)
    return jnp.concatenate([out[g * requests : (g + 1) * requests] for g in range(groups)], axis=1)


def pack_slots(routes, pages, slots):
    count = pages.shape[0]
    heads, cap = slots.shape[:2]
    dest = [routes[j] for j in range(count)]
    rank = []
    for j in range(count):
        r = jnp.int32(0)
        for i in range(j):
            r = r + (dest[i] == dest[j]).astype(jnp.int32)
        rank.append(r)
    key = [dest[j] * cap + rank[j] for j in range(count)]
    for h in range(heads):
        for k in range(cap):
            index, found = jnp.int32(0), jnp.int32(0)
            for j in range(count):
                hit = (key[j] == h * cap + k).astype(jnp.int32)
                index = index + hit * j
                found = found + hit
            page = pages[index]
            slots[h, k] = jnp.where(found > 0, page, jnp.zeros_like(page))


def kernel(
    chips,
    q_in,
    new_in,
    counts_in,
    fill_in,
    order_in,
    gain_in,
    routes_in,
    kv_in,
    hidden_in,
    weight_in,
    pages_in,
    arr,
    residual_ref,
    normed_ref,
    q_ref,
    new_ref,
    counts_ref,
    fill_ref,
    order_ref,
    gain_ref,
    routes_ref,
    kv,
    weight,
    hidden,
    pages,
    slots,
    gain_wide,
    scores,
    part,
    sibling_part,
    give,
    got_pair,
    terms,
    got_terms,
    blocks,
    load_sem,
    own_sem,
    page_send,
    near_sem,
    far_send,
    far_sem,
    partner_sem,
    core_send,
    core_sem,
    part_send,
    part_sem,
    pair_send,
    pair_sem,
    term_send,
    term_sem,
    block_send,
    block_near,
    block_relay,
    block_far,
    block_partner,
    share_send,
    share_sem,
    wave_two,
    wave_four,
):
    pairs = chips // 2
    reach = pairs // 2
    block = blocks.shape[3]
    a = lax.axis_index("heads")
    z, c = a // CORES, a % CORES
    pair, parity = z // 2, z % 2
    partner_z = z + 1 - 2 * parity
    sibling = z * CORES + (1 - c)

    def lane(zt):
        return zt * CORES + c

    def remote(src, dst, send, recv, dev):
        return pltpu.make_async_remote_copy(
            src_ref=src, dst_ref=dst, send_sem=send, recv_sem=recv, device_id={"heads": dev}, device_id_type=MESH
        )

    def chip_of(k, side):
        return 2 * ((pair + pairs + k) % pairs) + side

    def signal(sem, dev):
        pl.semaphore_signal(sem, inc=1, device_id={"heads": dev}, device_id_type=MESH)

    barrier = pltpu.get_barrier_semaphore()
    signal(barrier, sibling)
    signal(barrier, lane(partner_z))
    for k in (-1, 1):
        for side in (0, 1):
            signal(barrier, lane(chip_of(k, side)))

    own_column = pl.multiple_of((c * chips + z) * block, block)
    loads = {
        name: pltpu.make_async_copy(src, dst, load_sem.at[i])
        for i, (name, src, dst) in enumerate(
            (
                ("routes", routes_in, routes_ref),
                ("pages", pages_in, pages),
                ("q", q_in, q_ref),
                ("new", new_in, new_ref),
                ("counts", counts_in, counts_ref),
                ("fill", fill_in, fill_ref),
                ("order", order_in, order_ref),
                ("kv", kv_in, kv),
                ("weight", weight_in, weight),
                ("hidden", hidden_in.at[:, pl.ds(own_column, block)], hidden),
                ("gain", gain_in, gain_ref),
            )
        )
    }
    for copy in loads.values():
        copy.start()
    loads["routes"].wait()
    loads["pages"].wait()
    pack_slots(routes_ref, pages, slots)
    pl.semaphore_wait(barrier, 6)

    def wave(sem, k):
        signal(sem, lane(chip_of(k, parity)))
        signal(sem, lane(chip_of(-k, parity)))


    started = []

    def go(copy):
        copy.start()
        started.append(copy)

    own = pltpu.make_async_copy(slots.at[pair], arr.at[a], own_sem)
    own.start()
    go(remote(slots.at[pair], arr.at[a], page_send.at[0], partner_sem, lane(partner_z)))

    def clockwise(k):
        h = (pair + k) % pairs
        go(remote(slots.at[h], arr.at[a], page_send.at[2 * k - 1], near_sem.at[(k - 1) * 2 + parity], lane(2 * h)))

    def counter(k):
        h = (pair + pairs - k) % pairs
        go(remote(slots.at[h], arr.at[a], page_send.at[2 * k], near_sem.at[(k - 1) * 2 + parity], lane(2 * h + 1)))

    def opposite():
        h = (pair + reach) % pairs
        go(
            remote(
                slots.at[h],
                arr.at[a],
                page_send.at[2 * reach - 1],
                near_sem.at[2 * (reach - 1)],
                lane(2 * h + 1 - parity),
            )
        )

    def source(m, side):
        if m == 2 * (reach - 1):
            zs = 2 * ((pair + reach) % pairs) + 1 - side
        else:
            k, sp = m // 2 + 1, m % 2
            zs = 2 * ((pair + pairs + (2 * side - 1) * k) % pairs) + sp
        return zs

    def to_sibling(zs):
        row = arr.at[lane(zs)]
        go(remote(row, row, core_send.at[zs], core_sem.at[zs], sibling))

    def relay_near(m):
        zs = source(m, parity)
        row = arr.at[lane(zs)]
        remote(row, row, far_send.at[m], near_sem.at[m], lane(partner_z)).wait_recv()
        go(remote(row, row, far_send.at[m], far_sem.at[m], lane(partner_z)))
        to_sibling(zs)

    def take_far(m):
        zs = source(m, 1 - parity)
        row = arr.at[lane(zs)]
        remote(row, row, far_send.at[m], far_sem.at[m], lane(partner_z)).wait_recv()
        to_sibling(zs)

    exchange = remote(part.at[1 - c], sibling_part, part_send, part_sem, sibling)
    share = remote(blocks.at[c], blocks.at[c], share_send, share_sem, sibling)

    state = {}

    def attention_scores():
        for name in ("q", "new", "counts", "fill", "order"):
            loads[name].wait()
        limits = page_limits(counts_ref, fill_ref, order_ref, kv.shape[1])
        loads["kv"].wait()
        state["top"], state["fresh"] = attend_scores(q_ref, new_ref, kv, scores, limits)

    def attention():
        attn = attend_values(q_ref, new_ref, kv, scores, state["top"], state["fresh"])
        loads["weight"].wait()
        for half in range(CORES):

            def project(zz, _, half=half):
                columns = pl.ds(pl.multiple_of((half * chips + zz) * block, block), block)
                part[half, zz] = jnp.dot(attn, weight[:, columns], preferred_element_type=F32)
                return 0

            lax.fori_loop(0, chips, project, 0, unroll=4)
        own.wait()
        to_sibling(z)
        exchange.start()

    near = 2 * reach - 1

    def owner(m, side):
        if m == near - 1:
            return 2 * ((pair + reach) % pairs) + 1 - side
        return 2 * ((pair + pairs + (2 * side - 1) * (m // 2 + 1)) % pairs) + m % 2

    def core_sum(zt):
        return part[c, zt] + sibling_part[zt]

    pair_exchange = remote(give, got_pair, pair_send, pair_sem, lane(partner_z))

    def send_terms():
        exchange.wait_recv()
        for m in range(near):
            give[m] = core_sum(owner(m, 1 - parity)).astype(BF16)
        give[near] = core_sum(partner_z).astype(BF16)
        pair_exchange.start()

    def send_pair_terms():
        pair_exchange.wait_recv()
        for m in range(near):
            terms[m] = (core_sum(owner(m, parity)) + got_pair[m].astype(F32)).astype(BF16)
        for m in range(near):
            place = near - 1 if m == near - 1 else (1 - parity) * (reach - 1) + m // 2
            to = lane(owner(m, parity))
            go(remote(terms.at[m], got_terms.at[place], term_send.at[m], term_sem.at[place], to))

    def sum_terms():
        total = core_sum(z) + got_pair[near].astype(F32)
        for m in range(near):
            remote(terms.at[m], got_terms.at[m], term_send.at[m], term_sem.at[m], sibling).wait_recv()
            total = total + got_terms[m].astype(F32)
        loads["hidden"].wait()
        blocks[c, z] = (hidden[...].astype(F32) + total).astype(BF16)

    def send_block():
        mine = blocks.at[c, z]
        go(remote(mine, mine, block_send.at[near], block_partner, lane(partner_z)))
        for m in range(near):
            k = m // 2 + 1
            if m == near - 1:
                at, zt = near - 1, 2 * ((pair + reach) % pairs) + 1 - parity
            elif m % 2 == 0:
                at, zt = (k - 1) * 2 + parity, 2 * ((pair + k) % pairs)
            else:
                at, zt = (k - 1) * 2 + parity, 2 * ((pair + pairs - k) % pairs) + 1
            go(remote(mine, mine, block_send.at[m], block_near.at[at], lane(zt)))

    def relay_blocks():
        for m in range(near):
            theirs = blocks.at[c, source(m, parity)]
            remote(theirs, theirs, block_relay.at[m], block_near.at[m], sibling).wait_recv()
            go(remote(theirs, theirs, block_relay.at[m], block_far.at[m], lane(partner_z)))

    def share_blocks():
        theirs = blocks.at[c, partner_z]
        remote(theirs, theirs, block_send.at[near], block_partner, sibling).wait_recv()
        for m in range(near):
            theirs = blocks.at[c, source(m, 1 - parity)]
            remote(theirs, theirs, block_relay.at[m], block_far.at[m], sibling).wait_recv()
        share.start()

    def norm():
        remote(blocks.at[1 - c], blocks.at[1 - c], share_send, share_sem, sibling).wait_recv()

        def squares(b, acc):
            x = blocks[b // chips, b % chips].astype(F32)
            return acc + x * x

        width = CORES * chips * block
        acc = lax.fori_loop(0, CORES * chips, squares, jnp.zeros(blocks.shape[2:], F32), unroll=4)
        inverse = lax.rsqrt(jnp.sum(acc, axis=1, keepdims=True) / width + norm_epsilon)
        loads["gain"].wait()
        gain_wide[...] = gain_ref[...].astype(F32)
        lanes = gain_wide.shape[1]
        rows = block // lanes

        def finish(b, _):
            columns = pl.ds(pl.multiple_of(b * block, block), block)
            x = blocks[b // chips, b % chips]
            gain = jnp.concatenate([gain_wide[pl.ds(b * rows + i, 1), :] for i in range(rows)], axis=1)
            residual_ref[:, columns] = x
            normed_ref[:, columns] = (x.astype(F32) * inverse * gain).astype(BF16)
            return 0

        lax.fori_loop(0, CORES * chips, finish, 0, unroll=4)

    def take_partner():
        row = arr.at[lane(partner_z)]
        remote(row, row, page_send.at[0], partner_sem, sibling).wait_recv()
        to_sibling(partner_z)

    named = {
        "scores": attention_scores,
        "attention": attention,
        "tell2": lambda: wave(wave_two, 1),
        "know2": lambda: pl.semaphore_wait(wave_two, 2),
        "tell4": lambda: wave(wave_four, 2),
        "know4": lambda: pl.semaphore_wait(wave_four, 2),
        "terms": send_terms,
        "pair": send_pair_terms,
        "brelay": relay_blocks,
        "sum": sum_terms,
        "block": send_block,
        "share": share_blocks,
        "norm": norm,
        "partner": take_partner,
        "opposite": opposite,
    }
    numbered = {"cw": clockwise, "ccw": counter, "relay": relay_near, "far": take_far}
    for step in PLAN:
        if step in named:
            named[step]()
        else:
            word = step.rstrip("0123456789")
            numbered[word](int(step[len(word) :]))

    for i in range(chips):
        theirs = arr.at[i * CORES + 1 - c]
        remote(theirs, theirs, core_send.at[i], core_sem.at[i], sibling).wait_recv()
    exchange.wait_send()
    pair_exchange.wait_send()
    share.wait_send()
    for copy in started:
        copy.wait_send()


def per_device(
    queries,
    new_kv,
    kv_pool,
    page_counts,
    last_fill,
    page_order,
    hidden,
    out_weight,
    norm_gain,
    sectioned,
    routes,
):
    head_count = lax.axis_size("heads")
    chips = head_count // CORES
    requests, width = hidden.shape
    _, pool, page_size, kv_width = kv_pool.shape
    page_count = sectioned.shape[2]
    block = width // head_count
    pairs = chips // 2
    near = pairs - 1
    if pairs != KV_HEADS or pairs != 8 or new_kv.shape[0] != 1:
        raise ValueError("unexpected layout")
    vmem = pl.BlockSpec(memory_space=pltpu.VMEM)
    hbm = pl.BlockSpec(memory_space=pltpu.HBM)
    anywhere = pl.BlockSpec(memory_space=pl.ANY)
    dma = pltpu.SemaphoreType.DMA
    slot_shape = (PER_HEAD_CAP, page_size, kv_width)
    arrival, residual, normed = pl.pallas_call(
        functools.partial(kernel, chips),
        out_shape=(
            pltpu.VMEM((head_count, *slot_shape), BF16),
            jax.ShapeDtypeStruct((requests, width), BF16),
            jax.ShapeDtypeStruct((requests, width), BF16),
        ),
        in_specs=[hbm] * 11,
        out_specs=(anywhere, vmem, vmem),
        scratch_shapes=[
            pltpu.VMEM(queries.shape, BF16),
            pltpu.VMEM(new_kv.shape[1:], BF16),
            pltpu.VMEM(page_counts.shape, jnp.int32),
            pltpu.VMEM(last_fill.shape, jnp.int32),
            pltpu.VMEM(page_order.shape, jnp.int32),
            pltpu.VMEM((width // LANES, LANES), BF16),
            pltpu.SMEM((page_count,), jnp.int32),
            pltpu.VMEM((pool, page_size, kv_width), BF16),
            pltpu.VMEM(out_weight.shape, BF16),
            pltpu.VMEM((requests, block), BF16),
            pltpu.VMEM((page_count, page_size, kv_width), BF16),
            pltpu.VMEM((KV_HEADS, *slot_shape), BF16),
            pltpu.VMEM((width // LANES, LANES), F32),
            pltpu.VMEM((requests * queries.shape[1] * 2 // kv_width, pool * page_size), F32),
            pltpu.VMEM((CORES, chips, requests, block), F32),
            pltpu.VMEM((chips, requests, block), F32),
            pltpu.VMEM((near + 1, requests, block), BF16),
            pltpu.VMEM((near + 1, requests, block), BF16),
            pltpu.VMEM((near, requests, block), BF16),
            pltpu.VMEM((near, requests, block), BF16),
            pltpu.VMEM((CORES, chips, requests, block), BF16),
            dma((11,)),
            dma,
            dma((pairs,)),
            dma((near,)),
            dma((near,)),
            dma((near,)),
            dma,
            dma((chips,)),
            dma((chips,)),
            dma,
            dma,
            dma,
            dma,
            dma((near,)),
            dma((near,)),
            dma((near + 1,)),
            dma((near,)),
            dma((near,)),
            dma((near,)),
            dma,
            dma,
            dma,
            pltpu.SemaphoreType.REGULAR,
            pltpu.SemaphoreType.REGULAR,
        ],
        compiler_params=pltpu.CompilerParams(
            collective_id=0, has_side_effects=True, vmem_limit_bytes=40 * 1024 * 1024
        ),
    )(*[pltpu.with_memory_space_constraint(x, pltpu.HBM) for x in (
        queries,
        new_kv[0],
        page_counts,
        last_fill,
        page_order,
        norm_gain.reshape(width // LANES, LANES),
        routes.reshape(page_count),
        kv_pool[0],
        hidden,
        out_weight,
        sectioned[0, 0],
    )])
    return (residual, normed, arrival[None, None])


def solution(mesh):
    return jax.shard_map(
        per_device,
        mesh=mesh,
        in_specs=(
            P(("groups", "batch"), "heads"),
            P(("groups", "heads"), "batch", None),
            P(("groups", "heads"), "batch", None, None),
            P(("groups", "batch"), None),
            P(("groups", "batch"), None),
            P(("groups", "batch"), None),
            P(("groups", "batch"), None),
            P("heads", None),
            P(),
            P(("groups", "heads"), "batch", None, None, None),
            P(("groups", "heads"), "batch", None, None),
        ),
        out_specs=(
            P(("groups", "batch"), None),
            P(("groups", "batch"), None),
            P(("groups", "heads"), "batch", None, None, None, None),
        ),
        check_vma=False,
    )
```

profile of v0, /device:TPU:33, one launch (start us, length us, event | category | flops | bytes accessed | tf_op | source)
XLA Modules:
  0.0 95.6 jit_solution(5261091665351984808)
XLA Ops:
  0.6 91.5 %shard_map.130 = (bf16[32,2,128,256]{3,2,1,0:T(8,128)(2,1)S(1)}, bf16[16,8192]{1,0:T(8,128)(2,1)S(1)}, bf16[16,8192]{1,0:T(8,128)(2,1)S(1)}) custom-call(bf16[16,256]{1,0:T(8,128)(2,1)} %q_in.1, bf16[16,256]{1,0:T(8,128)(2,1)} %bitcast.10, s32[1,16]{1,0:T(1,128)} %counts_in.1, s32[1,16]{1,0:T(1,128)} %fill_in.1, s32[1,48]{1,0:T(1,128)} %order_in.1, ...), custom_call_target="tpu_custom_call" | custom-call | tf_op jit(solution)/shard_map/pallas_call | solution.py:512
  92.2 2.0 %copy.17 = bf16[1,1,32,2,128,256]{5,4,3,2,1,0:T(8,128)(2,1)} copy(bf16[1,1,32,2,128,256]{5,4,3,2,1,0:T(8,128)(2,1)S(1)} %bitcast.6) | data formatting | bytes 8388608
  94.2 0.7 copy.18
  94.9 0.7 copy.19
where the time goes:
time: 95.7 us; the launch traced here: 95.6 us
  Pallas kernels  91.5 us (96%)
  local copies, waits for them, and re-layouts  3.42 us (4%)
    pallas_call x1, Pallas kernels, per_device(): pl.pallas_call(functools.partial(kernel, chips), out_shape=(pltpu.VMEM((h...  91.5 us
    unnamed x3, local copies, waits for them, and re-layouts  3.42 us

commit v1 on v0

--- a/solution.py
+++ b/solution.py
@@ -12,42 +12,45 @@
 CORES = 2
 CHUNK_PAGES = 8
 LANES = 128
+ARRIVAL_COPIES = 4
 PLAN = (
-    "cw1",
-    "ccw1",
+    "toward1",
+    "away1",
     "tell2",
     "scores",
     "know2",
-    "cw2",
-    "ccw2",
+    "away2",
+    "toward2",
     "tell4",
     "attention",
     "know4",
     "terms",
+    "away3",
     "relay0",
     "relay1",
     "partner",
     "pair",
-    "cw3",
-    "ccw3",
+    "toward3",
     "relay2",
     "relay3",
+    "opposite",
     "sum",
     "block",
-    "opposite",
+    "relay4",
+    "relay5",
+    "brelay",
+    "relay6",
+    "relay7",
     "far0",
     "far1",
     "far2",
     "far3",
-    "relay4",
-    "relay5",
-    "brelay",
-    "relay6",
     "share",
-    "norm",
+    "shared",
     "far4",
     "far5",
     "far6",
+    "far7",
 )
 norm_epsilon = 1e-06
 
@@ -155,28 +158,24 @@
     counts_in,
     fill_in,
     order_in,
-    gain_in,
     routes_in,
     kv_in,
     hidden_in,
     weight_in,
     pages_in,
     arr,
-    residual_ref,
-    normed_ref,
+    blocks,
     q_ref,
     new_ref,
     counts_ref,
     fill_ref,
     order_ref,
-    gain_ref,
     routes_ref,
     kv,
     weight,
     hidden,
     pages,
     slots,
-    gain_wide,
     scores,
     part,
     sibling_part,
@@ -184,7 +183,6 @@
     got_pair,
     terms,
     got_terms,
-    blocks,
     load_sem,
     own_sem,
     page_send,
@@ -212,6 +210,8 @@
 ):
     pairs = chips // 2
     reach = pairs // 2
+    near = 2 * reach - 1
+    cap = slots.shape[1]
     block = blocks.shape[3]
     a = lax.axis_index("heads")
     z, c = a // CORES, a % CORES
@@ -255,7 +255,6 @@
                 ("kv", kv_in, kv),
                 ("weight", weight_in, weight),
                 ("hidden", hidden_in.at[:, pl.ds(own_column, block)], hidden),
-                ("gain", gain_in, gain_ref),
             )
         )
     }
@@ -281,50 +280,51 @@
     own.start()
     go(remote(slots.at[pair], arr.at[a], page_send.at[0], partner_sem, lane(partner_z)))
 
-    def clockwise(k):
-        h = (pair + k) % pairs
-        go(remote(slots.at[h], arr.at[a], page_send.at[2 * k - 1], near_sem.at[(k - 1) * 2 + parity], lane(2 * h)))
-
-    def counter(k):
-        h = (pair + pairs - k) % pairs
-        go(remote(slots.at[h], arr.at[a], page_send.at[2 * k], near_sem.at[(k - 1) * 2 + parity], lane(2 * h + 1)))
+    def toward(k):
+        h = (pair + pairs + (1 - 2 * parity) * k) % pairs
+        to = lane(2 * h + parity)
+        go(remote(slots.at[h], arr.at[a], page_send.at[2 * k - 1], near_sem.at[(k - 1) * 2 + parity], to))
+
+    def away(k):
+        h = (pair + pairs - (1 - 2 * parity) * k) % pairs
+        to = lane(2 * h + 1 - parity)
+        go(remote(slots.at[h], arr.at[a], page_send.at[2 * k], near_sem.at[(k - 1) * 2 + parity], to))
 
     def opposite():
         h = (pair + reach) % pairs
-        go(
-            remote(
-                slots.at[h],
-                arr.at[a],
-                page_send.at[2 * reach - 1],
-                near_sem.at[2 * (reach - 1)],
-                lane(2 * h + 1 - parity),
-            )
-        )
+        for k in range(cap):
+            m = near - 1 + k
+            to = lane(2 * h + 1 - parity)
+            go(remote(slots.at[h, k], arr.at[a, k], page_send.at[m + 1], near_sem.at[m], to))
 
     def source(m, side):
-        if m == 2 * (reach - 1):
-            zs = 2 * ((pair + reach) % pairs) + 1 - side
-        else:
-            k, sp = m // 2 + 1, m % 2
-            zs = 2 * ((pair + pairs + (2 * side - 1) * k) % pairs) + sp
-        return zs
+        if m >= near - 1:
+            return 2 * ((pair + reach) % pairs) + 1 - side
+        k, sp = m // 2 + 1, m % 2
+        return 2 * ((pair + pairs + (2 * side - 1) * k) % pairs) + sp
+
+    def arrived(m, side):
+        row = arr.at[lane(source(m, side))]
+        return row.at[m - near + 1] if m >= near - 1 else row
 
     def to_sibling(zs):
         row = arr.at[lane(zs)]
         go(remote(row, row, core_send.at[zs], core_sem.at[zs], sibling))
 
+    last_page = near + cap - 2
+
     def relay_near(m):
-        zs = source(m, parity)
-        row = arr.at[lane(zs)]
-        remote(row, row, far_send.at[m], near_sem.at[m], lane(partner_z)).wait_recv()
-        go(remote(row, row, far_send.at[m], far_sem.at[m], lane(partner_z)))
-        to_sibling(zs)
+        pages_ref = arrived(m, parity)
+        remote(pages_ref, pages_ref, far_send.at[m], near_sem.at[m], lane(partner_z)).wait_recv()
+        go(remote(pages_ref, pages_ref, far_send.at[m], far_sem.at[m], lane(partner_z)))
+        if m < near - 1 or m == last_page:
+            to_sibling(source(m, parity))
 
     def take_far(m):
-        zs = source(m, 1 - parity)
-        row = arr.at[lane(zs)]
-        remote(row, row, far_send.at[m], far_sem.at[m], lane(partner_z)).wait_recv()
-        to_sibling(zs)
+        pages_ref = arrived(m, 1 - parity)
+        remote(pages_ref, pages_ref, far_send.at[m], far_sem.at[m], lane(partner_z)).wait_recv()
+        if m < near - 1 or m == last_page:
+            to_sibling(source(m, 1 - parity))
 
     exchange = remote(part.at[1 - c], sibling_part, part_send, part_sem, sibling)
     share = remote(blocks.at[c], blocks.at[c], share_send, share_sem, sibling)
@@ -353,32 +353,39 @@
         to_sibling(z)
         exchange.start()
 
-    near = 2 * reach - 1
+    turned = (z + chips - 1) % chips
+    team, side_here = turned // 2, turned % 2
+
+    def member(k, side):
+        return (2 * ((team + pairs + k) % pairs) + side + 1) % chips
+
+    mate = lane(member(0, 1 - side_here))
+    mate_z = member(0, 1 - side_here)
 
     def owner(m, side):
         if m == near - 1:
-            return 2 * ((pair + reach) % pairs) + 1 - side
-        return 2 * ((pair + pairs + (2 * side - 1) * (m // 2 + 1)) % pairs) + m % 2
+            return member(reach, 1 - side)
+        return member((2 * side - 1) * (m // 2 + 1), m % 2)
 
     def core_sum(zt):
         return part[c, zt] + sibling_part[zt]
 
-    pair_exchange = remote(give, got_pair, pair_send, pair_sem, lane(partner_z))
+    pair_exchange = remote(give, got_pair, pair_send, pair_sem, mate)
 
     def send_terms():
         exchange.wait_recv()
         for m in range(near):
-            give[m] = core_sum(owner(m, 1 - parity)).astype(BF16)
-        give[near] = core_sum(partner_z).astype(BF16)
+            give[m] = core_sum(owner(m, 1 - side_here)).astype(BF16)
+        give[near] = core_sum(mate_z).astype(BF16)
         pair_exchange.start()
 
     def send_pair_terms():
         pair_exchange.wait_recv()
         for m in range(near):
-            terms[m] = (core_sum(owner(m, parity)) + got_pair[m].astype(F32)).astype(BF16)
+            terms[m] = (core_sum(owner(m, side_here)) + got_pair[m].astype(F32)).astype(BF16)
         for m in range(near):
-            place = near - 1 if m == near - 1 else (1 - parity) * (reach - 1) + m // 2
-            to = lane(owner(m, parity))
+            place = near - 1 if m == near - 1 else (1 - side_here) * (reach - 1) + m // 2
+            to = lane(owner(m, side_here))
             go(remote(terms.at[m], got_terms.at[place], term_send.at[m], term_sem.at[place], to))
 
     def sum_terms():
@@ -391,55 +398,33 @@
 
     def send_block():
         mine = blocks.at[c, z]
-        go(remote(mine, mine, block_send.at[near], block_partner, lane(partner_z)))
+        go(remote(mine, mine, block_send.at[near], block_partner, mate))
         for m in range(near):
             k = m // 2 + 1
             if m == near - 1:
-                at, zt = near - 1, 2 * ((pair + reach) % pairs) + 1 - parity
+                at, zt = near - 1, member(reach, 1 - side_here)
             elif m % 2 == 0:
-                at, zt = (k - 1) * 2 + parity, 2 * ((pair + k) % pairs)
+                at, zt = (k - 1) * 2 + side_here, member(k, 0)
             else:
-                at, zt = (k - 1) * 2 + parity, 2 * ((pair + pairs - k) % pairs) + 1
+                at, zt = (k - 1) * 2 + side_here, member(-k, 1)
             go(remote(mine, mine, block_send.at[m], block_near.at[at], lane(zt)))
 
     def relay_blocks():
         for m in range(near):
-            theirs = blocks.at[c, source(m, parity)]
+            theirs = blocks.at[c, owner(m, side_here)]
             remote(theirs, theirs, block_relay.at[m], block_near.at[m], sibling).wait_recv()
-            go(remote(theirs, theirs, block_relay.at[m], block_far.at[m], lane(partner_z)))
+            go(remote(theirs, theirs, block_relay.at[m], block_far.at[m], mate))
 
     def share_blocks():
-        theirs = blocks.at[c, partner_z]
+        theirs = blocks.at[c, mate_z]
         remote(theirs, theirs, block_send.at[near], block_partner, sibling).wait_recv()
         for m in range(near):
-            theirs = blocks.at[c, source(m, 1 - parity)]
+            theirs = blocks.at[c, owner(m, 1 - side_here)]
             remote(theirs, theirs, block_relay.at[m], block_far.at[m], sibling).wait_recv()
         share.start()
 
-    def norm():
+    def shared():
         remote(blocks.at[1 - c], blocks.at[1 - c], share_send, share_sem, sibling).wait_recv()
-
-        def squares(b, acc):
-            x = blocks[b // chips, b % chips].astype(F32)
-            return acc + x * x
-
-        width = CORES * chips * block
-        acc = lax.fori_loop(0, CORES * chips, squares, jnp.zeros(blocks.shape[2:], F32), unroll=4)
-        inverse = lax.rsqrt(jnp.sum(acc, axis=1, keepdims=True) / width + norm_epsilon)
-        loads["gain"].wait()
-        gain_wide[...] = gain_ref[...].astype(F32)
-        lanes = gain_wide.shape[1]
-        rows = block // lanes
-
-        def finish(b, _):
-            columns = pl.ds(pl.multiple_of(b * block, block), block)
-            x = blocks[b // chips, b % chips]
-            gain = jnp.concatenate([gain_wide[pl.ds(b * rows + i, 1), :] for i in range(rows)], axis=1)
-            residual_ref[:, columns] = x
-            normed_ref[:, columns] = (x.astype(F32) * inverse * gain).astype(BF16)
-            return 0
-
-        lax.fori_loop(0, CORES * chips, finish, 0, unroll=4)
 
     def take_partner():
         row = arr.at[lane(partner_z)]
@@ -459,11 +444,11 @@
         "sum": sum_terms,
         "block": send_block,
         "share": share_blocks,
-        "norm": norm,
+        "shared": shared,
         "partner": take_partner,
         "opposite": opposite,
     }
-    numbered = {"cw": clockwise, "ccw": counter, "relay": relay_near, "far": take_far}
+    numbered = {"toward": toward, "away": away, "relay": relay_near, "far": take_far}
     for step in PLAN:
         if step in named:
             named[step]()
@@ -479,6 +464,47 @@
     share.wait_send()
     for copy in started:
         copy.wait_send()
+
+
+def finish_kernel(arr, blocks, gain_in, arrival, residual_out, normed_out, gain_ref, gain_wide, residual, normed, sem):
+    parts = ARRIVAL_COPIES
+    rows = arr.shape[0] // parts
+    copies = [
+        pltpu.make_async_copy(arr.at[pl.ds(i * rows, rows)], arrival.at[pl.ds(i * rows, rows)], sem.at[i])
+        for i in range(parts)
+    ]
+    gain_copy = pltpu.make_async_copy(gain_in, gain_ref, sem.at[parts])
+    gain_copy.start()
+    for copy in copies:
+        copy.start()
+    halves, chips, requests, block = blocks.shape
+
+    def squares(b, acc):
+        x = blocks[b // chips, b % chips].astype(F32)
+        return acc + x * x
+
+    acc = lax.fori_loop(0, halves * chips, squares, jnp.zeros((requests, block), F32), unroll=8)
+    width = halves * chips * block
+    inverse = lax.rsqrt(jnp.sum(acc, axis=1, keepdims=True) / width + norm_epsilon)
+    gain_copy.wait()
+    gain_wide[...] = gain_ref[...].astype(F32)
+    per_block = block // gain_wide.shape[1]
+
+    def normalise(b, _):
+        columns = pl.ds(pl.multiple_of(b * block, block), block)
+        x = blocks[b // chips, b % chips]
+        gain = jnp.concatenate([gain_wide[pl.ds(b * per_block + i, 1), :] for i in range(per_block)], axis=1)
+        residual[:, columns] = x
+        normed[:, columns] = (x.astype(F32) * inverse * gain).astype(BF16)
+        return 0
+
+    lax.fori_loop(0, halves * chips, normalise, 0, unroll=8)
+    copies.append(pltpu.make_async_copy(residual, residual_out, sem.at[parts + 1]))
+    copies.append(pltpu.make_async_copy(normed, normed_out, sem.at[parts + 2]))
+    copies[-2].start()
+    copies[-1].start()
+    for copy in copies:
+        copy.wait()
 
 
 def per_device(
@@ -509,29 +535,26 @@
     anywhere = pl.BlockSpec(memory_space=pl.ANY)
     dma = pltpu.SemaphoreType.DMA
     slot_shape = (PER_HEAD_CAP, page_size, kv_width)
-    arrival, residual, normed = pl.pallas_call(
+    landed, blocks = pl.pallas_call(
         functools.partial(kernel, chips),
         out_shape=(
             pltpu.VMEM((head_count, *slot_shape), BF16),
-            jax.ShapeDtypeStruct((requests, width), BF16),
-            jax.ShapeDtypeStruct((requests, width), BF16),
+            pltpu.VMEM((CORES, chips, requests, block), BF16),
         ),
-        in_specs=[hbm] * 11,
-        out_specs=(anywhere, vmem, vmem),
+        in_specs=[hbm] * 10,
+        out_specs=(anywhere, vmem),
         scratch_shapes=[
             pltpu.VMEM(queries.shape, BF16),
             pltpu.VMEM(new_kv.shape[1:], BF16),
             pltpu.VMEM(page_counts.shape, jnp.int32),
             pltpu.VMEM(last_fill.shape, jnp.int32),
             pltpu.VMEM(page_order.shape, jnp.int32),
-            pltpu.VMEM((width // LANES, LANES), BF16),
             pltpu.SMEM((page_count,), jnp.int32),
             pltpu.VMEM((pool, page_size, kv_width), BF16),
             pltpu.VMEM(out_weight.shape, BF16),
             pltpu.VMEM((requests, block), BF16),
             pltpu.VMEM((page_count, page_size, kv_width), BF16),
             pltpu.VMEM((KV_HEADS, *slot_shape), BF16),
-            pltpu.VMEM((width // LANES, LANES), F32),
             pltpu.VMEM((requests * queries.shape[1] * 2 // kv_width, pool * page_size), F32),
             pltpu.VMEM((CORES, chips, requests, block), F32),
             pltpu.VMEM((chips, requests, block), F32),
@@ -539,13 +562,12 @@
             pltpu.VMEM((near + 1, requests, block), BF16),
             pltpu.VMEM((near, requests, block), BF16),
             pltpu.VMEM((near, requests, block), BF16),
-            pltpu.VMEM((CORES, chips, requests, block), BF16),
-            dma((11,)),
-            dma,
-            dma((pairs,)),
-            dma((near,)),
-            dma((near,)),
-            dma((near,)),
+            dma((10,)),
+            dma,
+            dma((near + PER_HEAD_CAP,)),
+            dma((near - 1 + PER_HEAD_CAP,)),
+            dma((near - 1 + PER_HEAD_CAP,)),
+            dma((near - 1 + PER_HEAD_CAP,)),
             dma,
             dma((chips,)),
             dma((chips,)),
@@ -574,13 +596,34 @@
         page_counts,
         last_fill,
         page_order,
-        norm_gain.reshape(width // LANES, LANES),
         routes.reshape(page_count),
         kv_pool[0],
         hidden,
         out_weight,
         sectioned[0, 0],
     )])
+    arrival, residual, normed = pl.pallas_call(
+        finish_kernel,
+        out_shape=(
+            jax.ShapeDtypeStruct((head_count, *slot_shape), BF16),
+            jax.ShapeDtypeStruct((requests, width), BF16),
+            jax.ShapeDtypeStruct((requests, width), BF16),
+        ),
+        in_specs=[vmem, vmem, hbm],
+        out_specs=(hbm, hbm, hbm),
+        scratch_shapes=[
+            pltpu.VMEM((width // LANES, LANES), BF16),
+            pltpu.VMEM((width // LANES, LANES), F32),
+            pltpu.VMEM((requests, width), BF16),
+            pltpu.VMEM((requests, width), BF16),
+            dma((ARRIVAL_COPIES + 3,)),
+        ],
+        compiler_params=pltpu.CompilerParams(vmem_limit_bytes=16 * 1024 * 1024),
+    )(
+        landed,
+        blocks,
+        pltpu.with_memory_space_constraint(norm_gain.reshape(width // LANES, LANES), pltpu.HBM),
+    )
     return (residual, normed, arrival[None, None])
 
 

time: 95.7 us -> 93.1 us (0.973)
  local copies, waits for them, and re-layouts: 3.42 us -> 0 us
    unnamed x3 -> x0, local copies, waits for them, and re-layouts: 3.42 us -> none
    pallas_call x0 -> x1, Pallas kernels: none -> 2.23 us  [per_device(): pl.pallas_call(finish_kernel, out_shape=(jax.ShapeDtypeStruct((head_count...]
    pallas_call x1, Pallas kernels: 91.5 us -> 90.1 us  [per_device(): pl.pallas_call(functools.partial(kernel, chips), out_shape=(pltpu.VMEM((h...]
where the time goes in v1:
time: 93.1 us; the launch traced here: 92.9 us
  Pallas kernels  92.3 us (99%)
    pallas_call x1, Pallas kernels, per_device(): pl.pallas_call(functools.partial(kernel, chips), out_shape=(pltpu.VMEM((h...  90.1 us
    pallas_call x1, Pallas kernels, per_device(): pl.pallas_call(finish_kernel, out_shape=(jax.ShapeDtypeStruct((head_count...  2.23 us

profile of v1, /device:TPU:33, one launch (start us, length us, event | category | flops | bytes accessed | tf_op | source)
XLA Modules:
  0.0 92.9 jit_solution(10174135557658109611)
XLA Ops:
  0.6 90.1 %shard_map.130 = (bf16[32,2,128,256]{3,2,1,0:T(8,128)(2,1)S(1)}, bf16[2,16,16,256]{3,2,1,0:T(8,128)(2,1)S(1)}) custom-call(bf16[16,256]{1,0:T(8,128)(2,1)} %q_in.1, bf16[16,256]{1,0:T(8,128)(2,1)} %bitcast.9, s32[1,16]{1,0:T(1,128)} %counts_in.1, s32[1,16]{1,0:T(1,128)} %fill_in.1, s32[1,48]{1,0:T(1,128)} %order_in.1, s32[8]{0:T(128)} %bitcast.10, ...), custom_call_target="tpu_custom_call" | custom-call | tf_op jit(solution)/shard_map/pallas_call | solution.py:538
  90.7 2.2 %shard_map.131 = (bf16[32,2,128,256]{3,2,1,0:T(8,128)(2,1)}, bf16[16,8192]{1,0:T(8,128)(2,1)}, bf16[16,8192]{1,0:T(8,128)(2,1)}) custom-call(bf16[32,2,128,256]{3,2,1,0:T(8,128)(2,1)S(1)} %get-tuple-element.8.arr, bf16[2,16,16,256]{3,2,1,0:T(8,128)(2,1)S(1)} %get-tuple-element.9.blocks, bf16[64,128]{1,0:T(8,128)(2,1)} %bitcast.8), custom_call_target="tpu_custom_call" | custom-call | tf_op jit(solution)/shard_map/pallas_call | solution.py:605

commit v2 on v1

--- a/solution.py
+++ b/solution.py
@@ -14,8 +14,8 @@
 LANES = 128
 ARRIVAL_COPIES = 4
 PLAN = (
+    "away1",
     "toward1",
-    "away1",
     "tell2",
     "scores",
     "know2",
@@ -38,9 +38,10 @@
     "block",
     "relay4",
     "relay5",
-    "brelay",
     "relay6",
     "relay7",
+    "brelay",
+    "brelast",
     "far0",
     "far1",
     "far2",
@@ -409,8 +410,8 @@
                 at, zt = (k - 1) * 2 + side_here, member(-k, 1)
             go(remote(mine, mine, block_send.at[m], block_near.at[at], lane(zt)))
 
-    def relay_blocks():
-        for m in range(near):
+    def relay_blocks(arrivals):
+        for m in arrivals:
             theirs = blocks.at[c, owner(m, side_here)]
             remote(theirs, theirs, block_relay.at[m], block_near.at[m], sibling).wait_recv()
             go(remote(theirs, theirs, block_relay.at[m], block_far.at[m], mate))
@@ -440,7 +441,8 @@
         "know4": lambda: pl.semaphore_wait(wave_four, 2),
         "terms": send_terms,
         "pair": send_pair_terms,
-        "brelay": relay_blocks,
+        "brelay": lambda: relay_blocks(range(4)),
+        "brelast": lambda: relay_blocks(range(4, near)),
         "sum": sum_terms,
         "block": send_block,
         "share": share_blocks,

time: 93.1 us -> 93.1 us (level)
  no operation moved by 1% of the time
where the time goes in v2:
time: 93.1 us; the launch traced here: 92.9 us
  Pallas kernels  92.3 us (99%)
    pallas_call x1, Pallas kernels, per_device(): pl.pallas_call(functools.partial(kernel, chips), out_shape=(pltpu.VMEM((h...  90.1 us
    pallas_call x1, Pallas kernels, per_device(): pl.pallas_call(finish_kernel, out_shape=(jax.ShapeDtypeStruct((head_count...  2.23 us

profile of v2, /device:TPU:33, one launch (start us, length us, event | category | flops | bytes accessed | tf_op | source)
XLA Modules:
  0.0 92.9 jit_solution(16135017361272254238)
XLA Ops:
  0.6 90.1 %shard_map.130 = (bf16[32,2,128,256]{3,2,1,0:T(8,128)(2,1)S(1)}, bf16[2,16,16,256]{3,2,1,0:T(8,128)(2,1)S(1)}) custom-call(bf16[16,256]{1,0:T(8,128)(2,1)} %q_in.1, bf16[16,256]{1,0:T(8,128)(2,1)} %bitcast.9, s32[1,16]{1,0:T(1,128)} %counts_in.1, s32[1,16]{1,0:T(1,128)} %fill_in.1, s32[1,48]{1,0:T(1,128)} %order_in.1, s32[8]{0:T(128)} %bitcast.10, ...), custom_call_target="tpu_custom_call" | custom-call | tf_op jit(solution)/shard_map/pallas_call | solution.py:540
  90.7 2.2 %shard_map.131 = (bf16[32,2,128,256]{3,2,1,0:T(8,128)(2,1)}, bf16[16,8192]{1,0:T(8,128)(2,1)}, bf16[16,8192]{1,0:T(8,128)(2,1)}) custom-call(bf16[32,2,128,256]{3,2,1,0:T(8,128)(2,1)S(1)} %get-tuple-element.8.arr, bf16[2,16,16,256]{3,2,1,0:T(8,128)(2,1)S(1)} %get-tuple-element.9.blocks, bf16[64,128]{1,0:T(8,128)(2,1)} %bitcast.8), custom_call_target="tpu_custom_call" | custom-call | tf_op jit(solution)/shard_map/pallas_call | solution.py:607
